TPU v7x, 32 devices: a whole 2x2x4 slice. The times are simulated.
32 devices in a mesh: expert: 16 (over z, y, x), width: 2 (over core).
Axes of the slice: x: 2, y: 2, z: 4, core: 2. Of those that a mesh axis runs over, the one named last changes fastest.
Arguments:
- tokens: bfloat16 [1024, 6144], P('expert', 'width'), may hold values from -6 to 6
- expert_ids: int32 [1024, 8], P('expert'), may hold values from 0 to 383, all different within a row; in each aligned block of 64 rows (0 to 63, 64 to 127, ...) at most 2 rows name the same one
- route_weight: float32 [1024, 8], P('expert'), may hold values from 0.2 to 1.5
- gate_weight: bfloat16 [16, 6144, 1024], P('expert', None, 'width'), may hold values from -0.078125 to 0.078125
- up_weight: bfloat16 [16, 6144, 1024], P('expert', None, 'width'), may hold values from -0.078125 to 0.078125
- down_weight: bfloat16 [16, 6144, 1024], P('expert', None, 'width'), may hold values from -0.1875 to 0.1875
Outputs:
- mixed: bfloat16 [1024, 6144], P('expert', 'width')
Inputs may be any that keep to these rules, and one draw needn't show every extreme that they name: `expert_ids`: each row names 8 different experts. In each aligned block of 64 rows (the rows of one index of the expert axis) no expert is named by more than 2 rows.
All inputs are finite; a program needn't handle non-finite values.
Results may differ from a plain program's by a relative error of at most 0.014.
Values may be sent and summed in bfloat16 or wider, within the bound.
No kernel may reach another device: no remote copies, remote signals or barrier semaphores. Data moves between devices by JAX's collectives and lax.ppermute only.
A program may use at most 64 MiB of HBM per device.

v0:
```python
import jax
import jax.numpy as jnp
from jax import lax
from jax.sharding import PartitionSpec as P

SEND = 2


def local_slots(route_ids, holders):
    experts_held = jnp.arange(holders, dtype=jnp.int32)
    route_hits = route_ids[:, :, None] == experts_held[None, None, :]
    matched = jnp.any(route_hits, axis=1).astype(jnp.int32)
    ranking = jnp.cumsum(matched, axis=0) - matched
    return (route_hits, matched, ranking)


def body(tokens, expert_ids, route_weight, gate_weight, up_weight, down_weight):
    holders = lax.axis_size("expert")
    tok_rows = tokens.shape[0]
    capacity = holders * SEND
    route_hits, matched, ranking = local_slots(expert_ids, holders)
    expert_base = jnp.arange(holders, dtype=jnp.int32)[None, :] * SEND
    slot_of = jnp.where(matched > 0, expert_base + ranking, capacity)
    row_number = jnp.broadcast_to(jnp.arange(tok_rows, dtype=jnp.int32)[:, None], slot_of.shape)
    slot_table = (
        jnp.full((capacity + 1,), tok_rows, jnp.int32)
        .at[slot_of.reshape(-1)]
        .set(row_number.reshape(-1))
    )
    outgoing = jnp.take(tokens, slot_table[:capacity], axis=0, mode="fill", fill_value=0)
    arrived = lax.all_to_all(
        outgoing.reshape(holders, SEND, outgoing.shape[1]),
        "expert",
        split_axis=0,
        concat_axis=0,
        tiled=True,
    )
    selected = arrived.reshape(capacity, arrived.shape[2])
    gate_mat = gate_weight[0]
    up_mat = up_weight[0]
    down_mat = down_weight[0]
    segment = lax.all_gather(selected, "width", axis=1, tiled=True)
    gate_val = jnp.dot(segment, gate_mat, preferred_element_type=jnp.float32)
    up_val = jnp.dot(segment, up_mat, preferred_element_type=jnp.float32)
    hidden = (jax.nn.silu(gate_val) * up_val).astype(jnp.bfloat16)
    weights_held = jnp.sum(jnp.where(route_hits, route_weight[:, :, None], 0.0), axis=1)
    slot_onehot = (ranking[:, :, None] == jnp.arange(SEND, dtype=jnp.int32)[None, None, :]) & (
        matched[:, :, None] > 0
    )
    coeff = (weights_held[:, :, None] * slot_onehot.astype(jnp.float32)).reshape(tok_rows, capacity)
    feature_rows = down_mat.shape[0] // lax.axis_size("width")
    summed = lax.psum_scatter(
        lax.dot_general(
            down_mat, hidden, (((1,), (1,)), ((), ())), preferred_element_type=jnp.float32
        ).astype(jnp.bfloat16),
        "width",
        scatter_dimension=0,
        tiled=True,
    ).astype(jnp.float32)
    returned = lax.all_to_all(
        summed.reshape(feature_rows, holders, SEND).astype(jnp.bfloat16),
        "expert",
        split_axis=1,
        concat_axis=1,
        tiled=True,
    ).astype(jnp.float32)
    returned = returned.reshape(feature_rows, capacity)
    combined = lax.dot_general(
        coeff,
        returned,
        (((1,), (1,)), ((), ())),
        precision=lax.Precision.HIGHEST,
        preferred_element_type=jnp.float32,
    )
    return combined.astype(jnp.bfloat16)


def solution(mesh):
    in_specs = (
        P("expert", "width"),
        P("expert", None),
        P("expert", None),
        P("expert", None, "width"),
        P("expert", None, "width"),
        P("expert", None, "width"),
    )
    out_specs = P("expert", "width")
    return jax.shard_map(body, mesh=mesh, in_specs=in_specs, out_specs=out_specs, check_vma=False)
```

profile of v0, /device:TPU:0, one launch (start us, length us, event | category | flops | bytes accessed | tf_op | source)
XLA Modules:
  0.0 75.9 jit_solution(6627106244274575018)
XLA Ops:
  6.5 0.0 copy-start
  6.5 0.0 reduce-scatter.2.cloned.1.call-start
  6.5 0.8 fusion.21
  7.3 0.1 copy.22
  7.4 0.1 reshape.111
  7.5 0.1 reduce_window_sum.11
  7.6 0.1 select_n.44
  7.7 4.3 %scatter_custom_fusion = s32[33]{0:T(128)S(1)} fusion(s32[1024]{0:T(1024)S(1)} %bitcast.27, s32[1024]{0:T(1024)S(1)} %reshape.111, s32[]{:T(128)} %constant.14.clone.1), kind=kCustom, calls=%fused_computation.40 | custom fusion | bytes 136 | tf_op jit(solution)/shard_map/scatter | solution.py:28
  12.0 0.1 slice.6
  12.1 0.0 copy-done
  12.2 0.7 gather_fusion
  12.8 0.1 gather.7
  12.9 0.3 broadcast_select_fusion
  13.2 16.8 %all_to_all.10 = bf16[16,2,3072]{2,1,0:T(2,128)(2,1)S(1)} all-to-all(bf16[16,2,3072]{2,1,0:T(2,128)(2,1)S(1)} %broadcast_select_fusion), channel_id=1, replica_groups=mesh['expert'=16,'width'=2] {'expert'}, dimensions={0} | all-to-all | bytes 393216 | tf_op jit(solution)/shard_map/all_to_all | solution.py:31
  30.0 0.1 reshape.98
  30.0 2.1 %all_gather.3 = bf16[32,6144]{1,0:T(8,128)(2,1)S(1)} all-gather(bf16[32,3072]{1,0:T(8,128)(2,1)S(1)} %reshape.98), channel_id=1, replica_groups=mesh['expert'=16,'width'=2] {'width'}, dimensions={1}, use_global_device_ids=true | all-gather | bytes 589824 | tf_op jit(solution)/shard_map/all_gather | solution.py:42
  32.1 3.9 %fusion.4 = f32[32,512]{1,0:T(8,128)S(1)} fusion(bf16[32,6144]{1,0:T(8,128)(2,1)S(1)} %all_gather.3, bf16[1,6144,512]{2,1,0:T(8,128)(2,1)} %param.9), kind=kOutput, calls=%fused_computation.7 | convolution fusion | flops 201326592 | bytes 6750208 | tf_op jit(solution)/shard_map/dot_general | solution.py:43
  36.1 0.0 copy-start.1
  36.1 0.0 copy-start.2
  36.1 8.4 %fusion = bf16[6144,32]{0,1:T(8,128)(2,1)} fusion(bf16[1,6144,512]{2,1,0:T(8,128)(2,1)} %param.11, bf16[32,6144]{1,0:T(8,128)(2,1)S(1)} %all_gather.3, bf16[1,6144,512]{2,1,0:T(8,128)(2,1)} %param.10, f32[32,512]{1,0:T(8,128)S(1)} %fusion.4), kind=kOutput, calls=%fused_computation.3 | convolution fusion | flops 402948096 | bytes 13434880 | tf_op jit(solution)/shard_map/dot_general | solution.py:53
  44.5 0.0 reduce-scatter.2.cloned.1.call-update
  44.5 5.7 %reduce-scatter.2.cloned.1.call-done = bf16[3072,32]{0,1:T(8,128)(2,1)} async-done(((bf16[6144,32]{0,1:T(8,128)(2,1)}), bf16[3072,32]{0,1:T(8,128)(2,1)}) %reduce-scatter.2.cloned.1.call-update) | async-done | bytes 196624 | tf_op jit(solution)/shard_map/reduce_scatter | solution.py:52
  50.2 1.7 %convert_element_type.42 = bf16[3072,16,2]{0,2,1:T(2,128)(2,1)} reshape(bf16[3072,32]{0,1:T(8,128)(2,1)} %reduce-scatter.2.cloned.1.call-done) | data formatting | bytes 393216 | tf_op jit(solution)/shard_map/convert_element_type | solution.py:61
  51.9 6.7 %all-to-all-start.1 = ((bf16[3072,16,2]{0,2,1:T(2,128)(2,1)}), bf16[3072,16,2]{0,2,1:T(2,128)(2,1)S(1)}, u32[]{:S(2)}, u32[]{:S(2)}) async-start(bf16[3072,16,2]{0,2,1:T(2,128)(2,1)} %convert_element_type.42), calls=%async_computation.2 | async-start | bytes 393216 | tf_op jit(solution)/shard_map/all_to_all | solution.py:60
  58.7 0.1 copy.24
  58.7 0.1 copy.23
  58.8 0.0 copy-done.1
  58.8 0.0 copy-done.2
  58.9 9.0 %all-to-all-done.1 = bf16[3072,16,2]{0,2,1:T(2,128)(2,1)S(1)} async-done(((bf16[3072,16,2]{0,2,1:T(2,128)(2,1)}), bf16[3072,16,2]{0,2,1:T(2,128)(2,1)S(1)}, u32[]{:S(2)}, u32[]{:S(2)}) %all-to-all-start.1) | async-done | bytes 196640 | tf_op jit(solution)/shard_map/all_to_all | solution.py:60
  67.8 1.3 %fusion.6 = bf16[64,3072]{1,0:T(8,128)(2,1)} fusion(bf16[3072,16,2]{0,2,1:T(2,128)(2,1)S(1)} %all-to-all-done.1, f32[64,16]{0,1:T(8,128)S(1)} %select_reduce_fusion, s32[64,16]{0,1:T(8,128)S(1)} %copy.23, pred[64,16]{0,1:T(8,128)(4,1)S(1)} %copy.24), kind=kOutput, calls=%fused_computation.10 | convolution fusion | flops 75700224 | bytes 599040 | tf_op jit(solution)/shard_map/dot_general | solution.py:68
  (9 shorter events, 0.1 us)
Async XLA Ops:
  6.5 5.6 %copy-start = (bf16[64,3072]{1,0:T(8,128)(2,1)S(1)}, bf16[64,3072]{1,0:T(8,128)(2,1)}, u32[]{:S(2)}) copy-start(bf16[64,3072]{1,0:T(8,128)(2,1)} %param.6) | copy-start | bytes 1179652
  6.5 43.7 %reduce-scatter.2.cloned.1.call-start = ((), (), s32[]{:S(2)}) async-start(), calls=%async_computation.3 | async-start | bytes 589824 | tf_op jit(solution)/shard_map/reduce_scatter | solution.py:52
  36.1 22.7 %copy-start.1 = (s32[64,8]{0,1:T(8,128)S(1)}, s32[64,8]{0,1:T(8,128)}, u32[]{:S(2)}) copy-start(s32[64,8]{0,1:T(8,128)} %param.7) | copy-start | bytes 6148
  36.1 22.7 %copy-start.2 = (f32[64,8]{0,1:T(8,128)S(1)}, f32[64,8]{0,1:T(8,128)}, u32[]{:S(2)}) copy-start(f32[64,8]{0,1:T(8,128)} %param.8) | copy-start | bytes 6148
  51.9 15.9 %all-to-all-start.1 = ((bf16[3072,16,2]{0,2,1:T(2,128)(2,1)}), bf16[3072,16,2]{0,2,1:T(2,128)(2,1)S(1)}, u32[]{:S(2)}, u32[]{:S(2)}) async-start(bf16[3072,16,2]{0,2,1:T(2,128)(2,1)} %convert_element_type.42), calls=%async_computation.2 | async-start | bytes 393216 | tf_op jit(solution)/shard_map/all_to_all | solution.py:60
Sparse Core Ops, SparseCore 0:
  44.6 5.5 reduce-scatter.1
where the time goes:
time: 76.2 us; the launch traced here: 75.9 us
  blocking collectives  18.9 us (25%)
  waiting for transfers between devices  14.7 us (19%)
  matrix products  13.6 us (18%)
  between operations  13.5 us (18%)
  local copies, waits for them, and re-layouts  7.31 us (10%)
  starting transfers between devices  6.74 us (9%)
  other arithmetic  1.2 us (2%)
    all_to_all x1, blocking collectives, body(): lax.all_to_all(outgoing.reshape(holders, SEND, outgoing.shape[1]), 'exper...  16.8 us
    all_to_all x1, waiting for transfers between devices, body(): lax.all_to_all(summed.reshape(feature_rows, holders, SEND).astype(jnp.bfl...  8.96 us
    dot_general x1, matrix products, body(): lax.dot_general(down_mat, hidden, (((1,), (1,)), ((), ())), preferred_ele...  8.41 us
    all_to_all x1, starting transfers between devices, body(): lax.all_to_all(summed.reshape(feature_rows, holders, SEND).astype(jnp.bfl...  6.74 us
    reduce_scatter x1, waiting for transfers between devices, body(): lax.psum_scatter(lax.dot_general(down_mat, hidden, (((1,), (1,)), ((), ()...  5.72 us
    scatter x1, local copies, waits for them, and re-layouts, body(): slot_table = jnp.full((capacity + 1,), tok_rows, jnp.int32).at[slot_of.re...  4.3 us
    dot_general x1, matrix products, body(): gate_val = jnp.dot(segment, gate_mat, preferred_element_type=jnp.float32)  3.94 us
    all_gather x1, blocking collectives, body(): segment = lax.all_gather(selected, 'width', axis=1, tiled=True)  2.09 us
  transfers between devices with their start and end apart: 2, of which 2 were waited for; matrix products, arithmetic and copies ran while one was open for 0% of the time, Pallas kernels for 0%

commit v1 on v0

--- a/solution.py
+++ b/solution.py
@@ -4,6 +4,14 @@
 from jax.sharding import PartitionSpec as P
 
 SEND = 2
+
+
+def _review_hubs(buf, mesh_ax):
+    t_next = lax.axis_size(mesh_ax)
+    then = jnp.split(buf, t_next, 1)
+    formed = jnp.stack(then, 0)
+    outer = lax.all_to_all(formed, axis_name=mesh_ax, split_axis=0, concat_axis=0)
+    return jnp.concatenate(outer, 1)
 
 
 def local_slots(route_ids, holders):
@@ -57,12 +65,8 @@
         scatter_dimension=0,
         tiled=True,
     ).astype(jnp.float32)
-    returned = lax.all_to_all(
-        summed.reshape(feature_rows, holders, SEND).astype(jnp.bfloat16),
-        "expert",
-        split_axis=1,
-        concat_axis=1,
-        tiled=True,
+    returned = _review_hubs(
+        summed.reshape(feature_rows, holders, SEND).astype(jnp.bfloat16), "expert"
     ).astype(jnp.float32)
     returned = returned.reshape(feature_rows, capacity)
     combined = lax.dot_general(

time: 76.2 us -> 85.4 us (1.12)
  local copies, waits for them, and re-layouts: 7.31 us -> 16.4 us
    unnamed x6 -> x21, local copies, waits for them, and re-layouts: 0.02 us -> 9.16 us
where the time goes in v1:
time: 85.4 us; the launch traced here: 85.1 us
  blocking collectives  18.9 us (22%)
  local copies, waits for them, and re-layouts  16.4 us (19%)
  waiting for transfers between devices  14.7 us (17%)
  matrix products  13.6 us (16%)
  between operations  13.5 us (16%)
  starting transfers between devices  6.74 us (8%)
  other arithmetic  1.22 us (1%)
    all_to_all x1, blocking collectives, body(): lax.all_to_all(outgoing.reshape(holders, SEND, outgoing.shape[1]), 'exper...  16.8 us
    unnamed x21, local copies, waits for them, and re-layouts  9.16 us
    all_to_all x1, waiting for transfers between devices, _review_hubs(): lax.all_to_all(formed, axis_name=mesh_ax, split_axis=0, concat_axis=0)  8.93 us
    dot_general x1, matrix products, body(): lax.dot_general(down_mat, hidden, (((1,), (1,)), ((), ())), preferred_ele...  8.41 us
    all_to_all x1, starting transfers between devices, _review_hubs(): lax.all_to_all(formed, axis_name=mesh_ax, split_axis=0, concat_axis=0)  6.74 us
    reduce_scatter x1, waiting for transfers between devices, body(): lax.psum_scatter(lax.dot_general(down_mat, hidden, (((1,), (1,)), ((), ()...  5.72 us
    scatter x1, local copies, waits for them, and re-layouts, body(): slot_table = jnp.full((capacity + 1,), tok_rows, jnp.int32).at[slot_of.re...  4.3 us
    dot_general x1, matrix products, body(): gate_val = jnp.dot(segment, gate_mat, preferred_element_type=jnp.float32)  3.94 us
  transfers between devices with their start and end apart: 2, of which 2 were waited for; matrix products, arithmetic and copies ran while one was open for 0% of the time, Pallas kernels for 0%

profile of v1, /device:TPU:0, one launch (start us, length us, event | category | flops | bytes accessed | tf_op | source)
XLA Modules:
  0.0 85.1 jit_solution(1261917490522471496)
XLA Ops:
  6.5 0.0 copy-start
  6.5 0.0 reduce-scatter.2.cloned.1.call-start
  6.5 0.8 fusion.19
  7.3 0.1 copy.13
  7.4 0.1 reshape.160
  7.5 0.1 reduce_window_sum.11
  7.6 0.1 select_n.44
  7.7 4.3 %scatter_custom_fusion = s32[33]{0:T(128)S(1)} fusion(s32[1024]{0:T(1024)S(1)} %bitcast.95, s32[1024]{0:T(1024)S(1)} %reshape.160, s32[]{:T(128)} %constant.14.clone.1), kind=kCustom, calls=%fused_computation.64 | custom fusion | bytes 136 | tf_op jit(solution)/shard_map/scatter | solution.py:36
  12.0 0.1 slice.6
  12.1 0.0 copy-done
  12.2 0.7 gather_fusion
  12.8 0.1 gather.7
  12.9 0.3 broadcast_select_fusion
  13.2 16.8 %all_to_all.10 = bf16[16,2,3072]{2,1,0:T(2,128)(2,1)S(1)} all-to-all(bf16[16,2,3072]{2,1,0:T(2,128)(2,1)S(1)} %broadcast_select_fusion), channel_id=1, replica_groups=mesh['expert'=16,'width'=2] {'expert'}, dimensions={0} | all-to-all | bytes 393216 | tf_op jit(solution)/shard_map/all_to_all | solution.py:39
  30.0 0.1 reshape.145
  30.0 2.1 %all_gather.3 = bf16[32,6144]{1,0:T(8,128)(2,1)S(1)} all-gather(bf16[32,3072]{1,0:T(8,128)(2,1)S(1)} %reshape.145), channel_id=1, replica_groups=mesh['expert'=16,'width'=2] {'width'}, dimensions={1}, use_global_device_ids=true | all-gather | bytes 589824 | tf_op jit(solution)/shard_map/all_gather | solution.py:50
  32.1 3.9 %fusion.4 = f32[32,512]{1,0:T(8,128)S(1)} fusion(bf16[32,6144]{1,0:T(8,128)(2,1)S(1)} %all_gather.3, bf16[1,6144,512]{2,1,0:T(8,128)(2,1)} %param.9), kind=kOutput, calls=%fused_computation.7 | convolution fusion | flops 201326592 | bytes 6750208 | tf_op jit(solution)/shard_map/dot_general | solution.py:51
  36.1 0.0 copy-start.1
  36.1 0.0 copy-start.2
  36.1 8.4 %fusion = bf16[6144,32]{0,1:T(8,128)(2,1)} fusion(bf16[1,6144,512]{2,1,0:T(8,128)(2,1)} %param.11, bf16[32,6144]{1,0:T(8,128)(2,1)S(1)} %all_gather.3, bf16[1,6144,512]{2,1,0:T(8,128)(2,1)} %param.10, f32[32,512]{1,0:T(8,128)S(1)} %fusion.4), kind=kOutput, calls=%fused_computation.3 | convolution fusion | flops 402948096 | bytes 13434880 | tf_op jit(solution)/shard_map/dot_general | solution.py:61
  44.5 0.0 reduce-scatter.2.cloned.1.call-update
  44.5 5.7 %reduce-scatter.2.cloned.1.call-done = bf16[3072,32]{0,1:T(8,128)(2,1)} async-done(((bf16[6144,32]{0,1:T(8,128)(2,1)}), bf16[3072,32]{0,1:T(8,128)(2,1)}) %reduce-scatter.2.cloned.1.call-update) | async-done | bytes 196624 | tf_op jit(solution)/shard_map/reduce_scatter | solution.py:60
  50.2 1.0 %convert_element_type.42 = bf16[3072,16,2]{0,2,1:T(2,128)(2,1)S(1)} reshape(bf16[3072,32]{0,1:T(8,128)(2,1)} %reduce-scatter.2.cloned.1.call-done) | data formatting | bytes 393216 | tf_op jit(solution)/shard_map/convert_element_type | solution.py:69
  51.2 0.6 constant_dynamic-update-slice_fusion.15
  51.9 0.6 constant_dynamic-update-slice_fusion.14
  52.5 0.6 constant_dynamic-update-slice_fusion.13
  53.1 0.6 constant_dynamic-update-slice_fusion.12
  53.7 0.6 constant_dynamic-update-slice_fusion.11
  54.3 0.6 constant_dynamic-update-slice_fusion.10
  54.9 0.6 constant_dynamic-update-slice_fusion.9
  55.5 0.6 constant_dynamic-update-slice_fusion.8
  56.1 0.6 constant_dynamic-update-slice_fusion.7
  56.7 0.6 constant_dynamic-update-slice_fusion.6
  57.3 0.6 constant_dynamic-update-slice_fusion.5
  58.0 0.6 constant_dynamic-update-slice_fusion.4
  58.6 0.6 constant_dynamic-update-slice_fusion.3
  59.2 0.6 constant_dynamic-update-slice_fusion.2
  59.8 0.6 constant_dynamic-update-slice_fusion.1
  60.4 0.6 constant_dynamic-update-slice_fusion
  61.0 6.7 %all-to-all-start.1 = ((bf16[16,3072,1,2]{1,3,2,0:T(2,128)(2,1)}), bf16[16,3072,1,2]{1,3,2,0:T(2,128)(2,1)S(1)}, u32[]{:S(2)}, u32[]{:S(2)}) async-start(bf16[16,3072,1,2]{1,3,2,0:T(2,128)(2,1)} %constant_dynamic-update-slice_fusion), calls=%async_computation.2 | async-start | bytes 393216 | tf_op jit(solution)/shard_map/all_to_all | solution.py:13
  67.8 0.1 copy.15
  67.8 0.1 copy.14
  67.9 0.0 copy-done.1
  67.9 0.0 copy-done.2
  68.0 8.9 %all-to-all-done.1 = bf16[16,3072,1,2]{1,3,2,0:T(2,128)(2,1)S(1)} async-done(((bf16[16,3072,1,2]{1,3,2,0:T(2,128)(2,1)}), bf16[16,3072,1,2]{1,3,2,0:T(2,128)(2,1)S(1)}, u32[]{:S(2)}, u32[]{:S(2)}) %all-to-all-start.1) | async-done | bytes 196640 | tf_op jit(solution)/shard_map/all_to_all | solution.py:13
  76.9 0.1 reshape.147
  77.0 1.3 %convolution_convert_fusion.1 = bf16[64,3072]{1,0:T(8,128)(2,1)} fusion(f32[64,32]{0,1:T(8,128)S(1)} %bitcast.94, bf16[3072,32]{0,1:T(8,128)(2,1)S(1)} %reshape.147), kind=kOutput, calls=%fused_computation.9 | convolution fusion | flops 75694080 | bytes 598016 | tf_op jit(solution)/shard_map/dot_general | solution.py:72
  (10 shorter events, 0.1 us)
Async XLA Ops:
  6.5 5.6 %copy-start = (bf16[64,3072]{1,0:T(8,128)(2,1)S(1)}, bf16[64,3072]{1,0:T(8,128)(2,1)}, u32[]{:S(2)}) copy-start(bf16[64,3072]{1,0:T(8,128)(2,1)} %param.6) | copy-start | bytes 1179652
  6.5 43.7 %reduce-scatter.2.cloned.1.call-start = ((), (), s32[]{:S(2)}) async-start(), calls=%async_computation.3 | async-start | bytes 589824 | tf_op jit(solution)/shard_map/reduce_scatter | solution.py:60
  36.1 31.8 %copy-start.1 = (s32[64,8]{0,1:T(8,128)S(1)}, s32[64,8]{0,1:T(8,128)}, u32[]{:S(2)}) copy-start(s32[64,8]{0,1:T(8,128)} %param.7) | copy-start | bytes 6148
  36.1 31.8 %copy-start.2 = (f32[64,8]{0,1:T(8,128)S(1)}, f32[64,8]{0,1:T(8,128)}, u32[]{:S(2)}) copy-start(f32[64,8]{0,1:T(8,128)} %param.8) | copy-start | bytes 6148
  61.0 15.9 %all-to-all-start.1 = ((bf16[16,3072,1,2]{1,3,2,0:T(2,128)(2,1)}), bf16[16,3072,1,2]{1,3,2,0:T(2,128)(2,1)S(1)}, u32[]{:S(2)}, u32[]{:S(2)}) async-start(bf16[16,3072,1,2]{1,3,2,0:T(2,128)(2,1)} %constant_dynamic-update-slice_fusion), calls=%async_computation.2 | async-start | bytes 393216 | tf_op jit(solution)/shard_map/all_to_all | solution.py:13
Sparse Core Ops, SparseCore 0:
  44.6 5.5 reduce-scatter.1
